TPU v7x, 256 devices: a whole 4x4x8 slice. The times are simulated.
256 devices in a mesh: seq: 64 (over x, z, y_lo), head: 4 (over y_hi, core).
Axes of the slice: x: 4, y: 4 (y_hi: 2, y_lo: 2; y = y_hi * 2 + y_lo), z: 8, core: 2. Of those that a mesh axis runs over, the one named last changes fastest.
Arguments:
- queries: bfloat16 [2, 512, 8192], P(None, 'seq', 'head'), may hold values from -256 to 256
- keys: bfloat16 [2, 16384, 1024], P(None, 'seq', 'head'), may hold values from -12 to 12
- lengths: int32 [2], replicated, may hold values from 768 to 16384, as said below
- starts: int32 [2], replicated, may hold values from 0 to 2048, as said below
Outputs:
- key_scores: float32 [2, 8, 16384], P(None, 'head', 'seq')
- token_scores: float32 [2, 16384], P(None, 'seq')
Inputs may be any that keep to these rules, and one draw needn't show every extreme that they name: `lengths`: every length is a multiple of 128 and at least 768; in every draw one request has length 16384. `starts`: each start is at most its request's length minus 512 minus 128; in every draw one start equals 2048.
All inputs are finite; a program needn't handle non-finite values.
Results may differ from a plain program's by a relative error of at most 0.0003.
Values may be sent and summed in bfloat16 or wider, within the bound.
A program may use at most 64 MiB of HBM per device.

v0:
```python
import jax
import jax.numpy as jnp
from jax import lax
from jax.sharding import Mesh
from jax.sharding import PartitionSpec as P

H = 64
KVH = 8
D = 128
QLEN = 512
SEQ = ("seq_0", "seq_1", "seq_2")


MASK_FILL = -1e30


def joined_along(blocks, dim):
    lengths = list(blocks.shape[1:])
    lengths[dim] *= blocks.shape[0]
    return jnp.moveaxis(blocks, 0, dim).reshape(lengths)


def all_blocks(value, axes, order):
    blocks = value
    for k in order:
        blocks = lax.all_gather(blocks, axes[k])
    done = order[::-1]
    back = [done.index(k) for k in range(len(axes))]
    blocks = blocks.transpose(*back, *range(len(axes), blocks.ndim))
    return blocks.reshape(-1, *value.shape)


def gathered_by_axis(value, axes, order, dim):
    return joined_along(all_blocks(value, axes, order), dim)


def merged_by_axis(value, axes, combine):
    for axis in axes:
        pieces = jax.tree.map(lambda part: lax.all_gather(part, axis), value)
        value = jax.tree.map(lambda part: part[0], pieces)
        for k in range(1, lax.axis_size(axis)):
            value = combine(value, jax.tree.map(lambda part: part[k], pieces))
    return value


def body(queries, keys, lengths, starts):
    requests = queries.shape[0]
    key_rows = keys.shape[1]
    heads_local = keys.shape[2] // D
    group_size = H // KVH
    score_scale = D ** (-0.5)
    cycle_index = lax.axis_index(SEQ)

    def merge_rows(earlier, later):
        row_top = jnp.maximum(earlier[0], later[0])
        row_total = earlier[1] * jnp.exp(earlier[0] - row_top) + later[1] * jnp.exp(
            later[0] - row_top
        )
        return (row_top, row_total)

    gathered = gathered_by_axis(queries, SEQ, (2, 0, 1), 1)
    all_block = gathered.reshape(requests, QLEN, heads_local, group_size, D)
    query_pos = lengths[:, None] - QLEN + jnp.arange(QLEN, dtype=jnp.int32)[None, :]
    piece_rows = keys.shape[1]
    key_block = keys.reshape(requests, piece_rows, heads_local, D)
    scores = (
        jnp.einsum("btghd,bkgd->bghtk", all_block, key_block, preferred_element_type=jnp.float32)
        * score_scale
    )
    key_pos = cycle_index * key_rows + jnp.arange(piece_rows, dtype=jnp.int32)
    allowed = (key_pos[None, None, None, None, :] <= query_pos[:, None, None, :, None]) & (
        key_pos[None, None, None, None, :] >= starts[:, None, None, None, None]
    )
    masked, allowed = (jnp.where(allowed, scores, MASK_FILL), allowed)
    local_top = jnp.max(masked, axis=4)
    local_total = jnp.sum(jnp.where(allowed, jnp.exp(masked - local_top[..., None]), 0.0), axis=4)
    row_top, row_total = merged_by_axis((local_top, local_total), SEQ, merge_rows)
    probs = jnp.where(allowed, jnp.exp(masked - row_top[..., None]), 0.0) / row_total[..., None]
    key_scores = jnp.sum(probs, axis=(2, 3))
    token_scores = lax.psum(jnp.sum(key_scores, axis=1), "head")
    return (key_scores, token_scores)


def solution(mesh):
    torus = Mesh(
        mesh.devices.reshape(4, 8, 2, mesh.shape["head"]), ("seq_0", "seq_1", "seq_2", "head")
    )
    in_specs = (P(None, SEQ, "head"), P(None, SEQ, "head"), P(), P())
    out_specs = (P(None, "head", SEQ), P(None, SEQ))
    return jax.shard_map(body, mesh=torus, in_specs=in_specs, out_specs=out_specs, check_vma=False)
```

profile of v0, /device:TPU:1, one launch (start us, length us, event | category | flops | bytes accessed | tf_op | source)
XLA Modules:
  0.0 204.5 jit_solution(3476993995718146357)
XLA Ops:
  7.2 0.0 all-gather.7.cloned.1.call-start
  7.2 4.7 %all-gather = bf16[4,8,2048]{2,1,0:T(8,128)(2,1)S(1)} all-gather(bf16[2,8,2048]{2,1,0:T(8,128)(2,1)} %param.4), channel_id=2, replica_groups=mesh['seq_0'=4,'seq_1'=8,'seq_2'=2,'head'=4] {'seq_2'}, dimensions={0}, use_global_device_ids=true | all-gather | bytes 196608 | tf_op jit(solution)/shard_map/all_gather | solution.py:26
  11.9 12.1 %all-gather.1 = bf16[8,2,8,2048]{3,2,1,0:T(8,128)(2,1)} all-gather(bf16[2,2,8,2048]{3,2,1,0:T(8,128)(2,1)S(1)} %bitcast.130), channel_id=3, replica_groups=mesh['seq_0'=4,'seq_1'=8,'seq_2'=2,'head'=4] {'seq_0'}, dimensions={0}, use_global_device_ids=true | all-gather | bytes 655360 | tf_op jit(solution)/shard_map/all_gather | solution.py:26
  24.0 0.0 all-gather.7.cloned.1.call-update
  24.1 1.0 reshape.104
  25.1 0.7 broadcast_add_fusion
  25.8 0.7 broadcast_compare_fusion
  26.5 0.1 iota_add_fusion
  26.6 0.2 compare_and_fusion
  26.8 57.7 %all-gather.7.cloned.1.call-done = bf16[32,2,2,8,2048]{4,3,2,1,0:T(8,128)(2,1)} async-done(((bf16[4,2,2,8,2048]{4,3,2,1,0:T(8,128)(2,1)}), bf16[32,2,2,8,2048]{4,3,2,1,0:T(8,128)(2,1)}) %all-gather.7.cloned.1.call-update) | async-done | bytes 4194320 | tf_op jit(solution)/shard_map/all_gather | solution.py:26
  84.6 2.5 %copy.14 = bf16[4,8,2,2,8,2048]{5,4,3,2,1,0:T(8,128)(2,1)S(1)} copy(bf16[4,8,2,2,8,2048]{5,4,3,2,0,1:T(8,128)(2,1)} %bitcast.127) | data formatting | bytes 8388608 | tf_op jit(solution)/shard_map/transpose | solution.py:29
  87.1 0.6 copy.15
  87.6 1.4 copy.21
  89.1 4.6 %fusion = (f32[2,2,8,512]{3,2,1,0:T(8,128)S(1)}, f32[2,2,256,512,8]{3,2,4,1,0:T(8,128)S(1)}) fusion(pred[2,512,256]{1,2,0:T(8,128)(4,1)S(1)} %compare_and_fusion, bf16[2,512,2,8,128]{4,3,2,1,0:T(8,128)(2,1)S(1)} %bitcast.126, bf16[2,256,2,128,1]{3,2,1,0,4:T(2,128)(2,1)S(1)} %bitcast.129), kind=kOutput, calls=%fused_computation.3 | convolution fusion | flops 1086308352 | bytes 21561344 | tf_op jit(solution)/shard_map/btghd,bkgd->bghtk/dot_general | solution.py:67
  93.7 10.4 %all-gather.3 = f32[8,2,8,512]{3,2,1,0:T(8,128)S(1)} all-gather(f32[2,2,8,512]{3,2,1,0:T(8,128)S(1)} %get-tuple-element.10), channel_id=5, replica_groups=mesh['seq_0'=4,'seq_1'=8,'seq_2'=2,'head'=4] {'seq_0'}, dimensions={0}, use_global_device_ids=true | all-gather | bytes 327680 | tf_op jit(solution)/shard_map/all_gather | solution.py:39
  104.1 4.1 %select_reduce_fusion = f32[2,2,8,512]{3,2,1,0:T(8,128)S(1)} fusion(f32[2,2,256,512,8]{3,2,4,1,0:T(8,128)S(1)} %get-tuple-element.11, f32[2,2,8,512]{3,2,1,0:T(8,128)S(1)} %get-tuple-element.10, pred[2,512,256]{1,2,0:T(8,128)(4,1)S(1)} %compare_and_fusion), kind=kLoop, calls=%fused_computation.1 | loop fusion | flops 20955136 | bytes 17170432 | tf_op jit(solution)/shard_map/reduce_sum | solution.py:76
  108.1 9.4 %all-gather.4 = f32[8,2,8,512]{3,2,1,0:T(8,128)S(1)} all-gather(f32[2,2,8,512]{3,2,1,0:T(8,128)S(1)} %select_reduce_fusion), channel_id=6, replica_groups=mesh['seq_0'=4,'seq_1'=8,'seq_2'=2,'head'=4] {'seq_0'}, dimensions={0}, use_global_device_ids=true | all-gather | bytes 327680 | tf_op jit(solution)/shard_map/all_gather | solution.py:39
  117.5 0.1 fusion.23
  117.6 19.7 %all_gather.58 = f32[8,2,2,8,512]{4,3,2,1,0:T(8,128)S(1)} all-gather(f32[1,2,2,8,512]{4,3,2,1,0:T(8,128)S(1)} %get-tuple-element.8), channel_id=1, replica_groups=mesh['seq_0'=4,'seq_1'=8,'seq_2'=2,'head'=4] {'seq_1'}, dimensions={0}, use_global_device_ids=true | all-gather | bytes 589824 | tf_op jit(solution)/shard_map/all_gather | solution.py:39
  137.3 19.8 %all_gather.54 = f32[8,2,2,8,512]{4,3,2,1,0:T(8,128)S(1)} all-gather(f32[1,2,2,8,512]{4,3,2,1,0:T(8,128)S(1)} %get-tuple-element.9), channel_id=1, replica_groups=mesh['seq_0'=4,'seq_1'=8,'seq_2'=2,'head'=4] {'seq_1'}, dimensions={0}, use_global_device_ids=true | all-gather | bytes 589824 | tf_op jit(solution)/shard_map/all_gather | solution.py:39
  157.2 0.2 fusion.9
  157.3 3.8 %all_gather.59 = f32[2,2,2,8,512]{4,3,2,1,0:T(8,128)S(1)} all-gather(f32[1,2,2,8,512]{4,3,2,1,0:T(8,128)S(1)} %get-tuple-element.6), channel_id=1, replica_groups=mesh['seq_0'=4,'seq_1'=8,'seq_2'=2,'head'=4] {'seq_2'}, dimensions={0}, use_global_device_ids=true | all-gather | bytes 196608 | tf_op jit(solution)/shard_map/all_gather | solution.py:39
  161.1 3.8 %all_gather.55 = f32[2,2,2,8,512]{4,3,2,1,0:T(8,128)S(1)} all-gather(f32[1,2,2,8,512]{4,3,2,1,0:T(8,128)S(1)} %get-tuple-element.7), channel_id=1, replica_groups=mesh['seq_0'=4,'seq_1'=8,'seq_2'=2,'head'=4] {'seq_2'}, dimensions={0}, use_global_device_ids=true | all-gather | bytes 196608 | tf_op jit(solution)/shard_map/all_gather | solution.py:39
  164.9 6.4 %fusion.3 = (f32[2,256]{1,0:T(2,128)S(1)}, f32[2,2,256]{2,1,0:T(2,128)}) fusion(f32[2,2,8,512]{3,2,1,0:T(8,128)S(1)} %get-tuple-element.4, f32[2,2,8,512]{3,2,1,0:T(8,128)S(1)} %get-tuple-element.5, f32[2,2,256,512,8]{3,2,4,1,0:T(8,128)S(1)} %get-tuple-element.11, pred[2,512,256]{1,2,0:T(8,128)(4,1)S(1)} %compare_and_fusion), kind=kLoop, calls=%fused_computation.6 | loop fusion | flops 29358592 | bytes 17176576 | tf_op jit(solution)/shard_map/reduce_sum | solution.py:80
  171.4 26.3 %psum.7 = f32[2,256]{1,0:T(2,128)} all-reduce(f32[2,256]{1,0:T(2,128)S(1)} %get-tuple-element.2), channel_id=1, replica_groups=mesh['seq_0'=4,'seq_1'=8,'seq_2'=2,'head'=4] {'head'}, use_global_device_ids=true, to_apply=%region_4.5 | all-reduce | flops 512 | bytes 4096 | tf_op jit(solution)/shard_map/psum | solution.py:80
  (2 shorter events, 0.0 us)
Async XLA Ops:
  7.2 77.4 %all-gather.7.cloned.1.call-start = ((), (), s32[]{:S(2)}) async-start(), calls=%async_computation | async-start | bytes 4718592 | tf_op jit(solution)/shard_map/all_gather | solution.py:26
Sparse Core Ops, SparseCore 0:
  24.2 60.3 all-gather.6
where the time goes:
time: 205 us
  blocking collectives  110 us (54%)
  waiting for transfers between devices  57.8 us (28%)
  between operations  14.1 us (7%)
  other arithmetic  12.5 us (6%)
  local copies, waits for them, and re-layouts  5.49 us (3%)
  matrix products  4.62 us (2%)
    all_gather x6, blocking collectives, merged_by_axis(): pieces = jax.tree.map(lambda part: lax.all_gather(part, axis), value)  66.9 us
    all_gather x1, waiting for transfers between devices, all_blocks(): blocks = lax.all_gather(blocks, axes[k])  57.7 us
    psum x1, blocking collectives, body(): token_scores = lax.psum(jnp.sum(key_scores, axis=1), 'head')  26.3 us
    all_gather x2, blocking collectives, all_blocks(): blocks = lax.all_gather(blocks, axes[k])  16.8 us
    reduce_sum x1, other arithmetic, body(): token_scores = lax.psum(jnp.sum(key_scores, axis=1), 'head')  6.44 us
    dot_general x1, matrix products, body(): jnp.einsum('btghd,bkgd->bghtk', all_block, key_block, preferred_element_t...  4.62 us
  transfers between devices with their start and end apart: 1, of which 1 were waited for; matrix products, arithmetic and copies ran while one was open for 1% of the time, Pallas kernels for 0%

commit v1 on v0

v1 whole, which is shorter than its diff:
```python
import functools
import math

import jax
import jax.numpy as jnp
from jax import lax
from jax.experimental import pallas as pl
from jax.experimental.pallas import tpu as pltpu
from jax.sharding import Mesh
from jax.sharding import PartitionSpec as P

H = 64
KVH = 8
D = 128
QLEN = 512
SEQ = ("seq_0", "seq_1", "seq_2")
AXES = SEQ + ("head",)
NX, NZ, NY, NH = 4, 8, 2, 4
TOK = 8
KEYS = 256
HALF = H // KVH // NY
ROWS = NX * NY * TOK * HALF
BLOCKS = NX * NY
FILL = -1e30
SCALE2 = D**-0.5 * math.log2(math.e)
MESH = pl.DeviceIdType.MESH
PLANE = tuple((dx, dy) for dx in (2, 1, 3, 0) for dy in (1, 0) if (dx, dy) != (0, 0))
OFFSETS = (0, 1, -1, 2, -2, 3, -3, 4)
ARRIVAL = {off: j for j, off in enumerate(OFFSETS)}
PIECES = 2
PX = NX // PIECES


def wrap(value, size):
    return lax.rem(value + size, size)


def kernel(
    len_ref, start_ref, q_hbm, k_hbm, key_out, tok_out,
    qloc, kloc, qbuf, kbuf, sbuf, thr, mrow, wrow, lse, part, got, tok,
    loc_sem, qs, qr, ks, kr, zs, zr, ss, sr, ps, pr, ts, tr,
):
    x, z, y, hd = (lax.axis_index(a) for a in AXES)
    f32 = jnp.float32

    def share_of(ref, px, py):
        b, g = px // 2, lax.rem(px, 2)
        lanes = pl.multiple_of(g * (NY * HALF * D) + py * (HALF * D), HALF * D)
        return ref.at[b, :, pl.ds(lanes, HALF * D)]

    def keys_of(ref, px):
        b, g = px // 2, lax.rem(px, 2)
        return ref.at[b, :, pl.ds(pl.multiple_of(g * D, D), D)]

    local = [
        pltpu.make_async_copy(q_hbm, qloc, loc_sem.at[0]),
        pltpu.make_async_copy(k_hbm, kloc, loc_sem.at[1]),
        pltpu.make_async_copy(share_of(q_hbm, x, y), qbuf.at[z, x, y], loc_sem.at[2]),
        pltpu.make_async_copy(keys_of(k_hbm, x), kbuf.at[x, y], loc_sem.at[3]),
    ]
    for copy in local:
        copy.start()

    barrier = pltpu.get_barrier_semaphore()
    partners = [(wrap(x + dx, NX), z, wrap(y + dy, NY), hd) for dx, dy in PLANE]
    partners += [(x, wrap(z + dz, NZ), y, hd) for dz in (2, -2, 1, -1)]
    partners += [(x, z, y, wrap(hd + dh, NH)) for dh in range(1, NH)]
    for partner in partners:
        pl.semaphore_signal(barrier, inc=1, device_id=partner, device_id_type=MESH)
    local[0].wait()
    local[1].wait()
    pl.semaphore_wait(barrier, len(partners))

    def remote(src, dst, send, recv, device):
        return pltpu.make_async_remote_copy(
            src_ref=src, dst_ref=dst, send_sem=send, recv_sem=recv,
            device_id=device, device_id_type=MESH,
        )

    started = []

    def start(copy):
        copy.start()
        started.append(copy)

    for n, (dx, dy) in enumerate(PLANE):
        px, py = wrap(x + dx, NX), wrap(y + dy, NY)
        start(remote(share_of(qloc, px, py), qbuf.at[z, x, y], qs.at[n], qr.at[x, y], (px, z, py, hd)))
    for n, (dx, dy) in enumerate(PLANE):
        px, py = wrap(x + dx, NX), wrap(y + dy, NY)
        start(remote(keys_of(kloc, px), kbuf.at[x, y], ks.at[n], kr.at[x, y], (px, z, py, hd)))

    b = x // 2
    start_pos = start_ref[b]
    for px in range(NX):
        for py in range(NY):
            pos = ((px * NZ + z) * NY + py) * KEYS + lax.broadcasted_iota(jnp.int32, (KEYS, D), 0)
            thr[px * NY + py] = jnp.where(pos >= start_pos, pos, jnp.int32(2**30))

    def z_copy(off, piece, dz, n):
        slot = wrap(z + off, NZ)
        rows = pl.ds(piece * PX, PX)
        there = off - dz
        j = ARRIVAL[there] if there in ARRIVAL else ARRIVAL[-there]
        return remote(
            qbuf.at[slot, rows], qbuf.at[slot, rows], zs.at[n], zr.at[j, piece],
            (x, wrap(z + dz, NZ), y, hd),
        )

    def z_wait(off, piece):
        slot = wrap(z + off, NZ)
        rows = pl.ds(piece * PX, PX)
        remote(
            qbuf.at[slot, rows], qbuf.at[slot, rows], zs.at[0], zr.at[ARRIVAL[off], piece],
            (x, wrap(z + 1, NZ), y, hd),
        ).wait_recv()

    for dx, dy in PLANE:
        px, py = wrap(x + dx, NX), wrap(y + dy, NY)
        remote(
            share_of(qloc, px, py), qbuf.at[z, px, py], qs.at[0], qr.at[px, py], (px, z, py, hd)
        ).wait_recv()
    local[2].wait()
    sends = 0
    for piece in range(PIECES):
        for dz in (1, -1):
            start(z_copy(0, piece, dz, sends))
            sends += 1
    for hop in (1, 2):
        for piece in range(PIECES):
            for side in (1, -1):
                z_wait(side * hop, piece)
                start(z_copy(side * hop, piece, -side, sends))
                sends += 1
                if hop == 2 and piece == (0 if side == -1 else PIECES - 1):
                    start(z_copy(side * hop, piece, -2 * side, sends))
                    sends += 1

    local[3].wait()
    for dx, dy in PLANE:
        px, py = wrap(x + dx, NX), wrap(y + dy, NY)
        remote(
            keys_of(kloc, px), kbuf.at[px, py], ks.at[0], kr.at[px, py], (px, z, py, hd)
        ).wait_recv()

    first_pos = len_ref[b] - QLEN

    def score(off):
        c = wrap(z + off, NZ)
        wide = qbuf[c].astype(f32).reshape(BLOCKS * TOK, HALF * D)
        q = jnp.concatenate([wide[:, h * D:(h + 1) * D] for h in range(HALF)], axis=0).astype(jnp.bfloat16)
        lane = lax.rem(lax.broadcasted_iota(jnp.int32, (1, ROWS), 1), BLOCKS * TOK)
        inner = NY * TOK
        query_pos = first_pos + (lane // inner) * (NZ * inner) + c * inner + lax.rem(lane, inner)

        def scores(n, top):
            s = lax.dot_general(
                kbuf[n // NY, lax.rem(n, NY)], q, (((1,), (1,)), ((), ())), preferred_element_type=f32
            )
            limit = thr[n]
            s = jnp.where(jnp.concatenate([limit, limit], axis=1) <= query_pos, s, FILL)
            sbuf[c, n] = s
            return jnp.maximum(top, jnp.max(s.reshape(KEYS // 8, 8, ROWS), axis=0))

        top = lax.fori_loop(0, BLOCKS, scores, jnp.full((8, ROWS), FILL, f32))
        top = jnp.max(top, axis=0, keepdims=True)

        def expos(n, total):
            e = jnp.exp2((sbuf[c, n] - top) * SCALE2)
            sbuf[c, n] = e
            return total + jnp.sum(e.reshape(KEYS // 8, 8, ROWS), axis=0)

        total = lax.fori_loop(0, BLOCKS, expos, jnp.zeros((8, ROWS), f32))
        total = jnp.sum(total, axis=0, keepdims=True)
        top = top * SCALE2
        mrow[pl.ds(c, 1), :] = top
        lse[z, pl.ds(c, 1), :] = top + jnp.log2(total)

    for off in OFFSETS:
        if abs(off) > 2:
            for piece in range(PIECES):
                z_wait(off, piece)
        score(off)

    def stats(dz, n):
        return remote(lse.at[z], lse.at[z], ss.at[n], sr.at[z], (x, wrap(z + dz, NZ), y, hd))

    for n, dz in enumerate((4, 3, -3, 2, -2, 1, -1)):
        start(stats(dz, n))
    for n, dz in enumerate((1, -1, 2, -2, 3, -3, 4)):
        other = wrap(z + dz, NZ)
        remote(lse.at[other], lse.at[other], ss.at[0], sr.at[other], (x, other, y, hd)).wait_recv()
    every = [lse[k] for k in range(NZ)]
    peak = functools.reduce(jnp.maximum, every)
    whole = peak + jnp.log2(sum(jnp.exp2(v - peak) for v in every))
    wrow[...] = jnp.exp2(mrow[...] - whole)

    ones = jnp.ones((16, D), jnp.bfloat16)
    order = PLANE + ((0, 0),)
    for n, (dx, dy) in enumerate(order):
        px, py = wrap(x + dx, NX), wrap(y + dy, NY)
        block = px * NY + py

        def weigh(c, acc):
            w = wrow[pl.ds(c, 1), :]
            e = sbuf[c, block] * w
            return acc + e[:, :D] + e[:, D:]

        acc = lax.fori_loop(0, NZ, weigh, jnp.zeros((KEYS, D), f32))
        hi = acc.astype(jnp.bfloat16)
        rest = acc - hi.astype(f32)
        mid = rest.astype(jnp.bfloat16)
        low = (rest - mid.astype(f32)).astype(jnp.bfloat16)
        sums = sum(
            lax.dot_general(ones, v, (((1,), (1,)), ((), ())), preferred_element_type=f32)
            for v in (low, mid, hi)
        )[0:1]
        if (dx, dy) == (0, 0):
            got[x, y] = sums
        else:
            part[n] = sums
            start(remote(part.at[n], got.at[x, y], ps.at[n], pr.at[x, y], (px, z, py, hd)))
    for n, (dx, dy) in enumerate(PLANE):
        px, py = wrap(x + dx, NX), wrap(y + dy, NY)
        remote(part.at[n], got.at[px, py], ps.at[n], pr.at[px, py], (px, z, py, hd)).wait_recv()

    heads = KVH // NH
    for request in range(2):
        sums = []
        for g in range(heads):
            pair = request * heads + g
            sums.append(got[pair, 0] + got[pair, 1])
            key_out[request, g:g + 1] = sums[-1]
        tok[hd, request] = sum(sums[1:], sums[0])
    for dh in range(1, NH):
        start(remote(tok.at[hd], tok.at[hd], ts.at[dh], tr.at[hd], (x, z, y, wrap(hd + dh, NH))))
    for dh in range(1, NH):
        other = wrap(hd + dh, NH)
        remote(tok.at[other], tok.at[other], ts.at[dh], tr.at[other], (x, z, y, other)).wait_recv()
    for request in range(2):
        tok_out[request:request + 1] = sum((tok[k, request] for k in range(1, NH)), tok[0, request])

    for copy in started:
        copy.wait_send()


def body(queries, keys, lengths, starts):
    f32, bf16 = jnp.float32, jnp.bfloat16
    dma = pltpu.SemaphoreType.DMA
    vmem = pltpu.VMEM
    return pl.pallas_call(
        kernel,
        out_shape=(
            jax.ShapeDtypeStruct((2, KVH // NH, KEYS), f32),
            jax.ShapeDtypeStruct((2, KEYS), f32),
        ),
        in_specs=[pl.BlockSpec(memory_space=pltpu.SMEM)] * 2
        + [pl.BlockSpec(memory_space=pltpu.HBM)] * 2,
        out_specs=(pl.BlockSpec(memory_space=vmem), pl.BlockSpec(memory_space=vmem)),
        scratch_shapes=[
            vmem(queries.shape, bf16),
            vmem(keys.shape, bf16),
            vmem((NZ, NX, NY, TOK, HALF * D), bf16),
            vmem((NX, NY, KEYS, D), bf16),
            vmem((NZ, BLOCKS, KEYS, ROWS), f32),
            vmem((BLOCKS, KEYS, D), jnp.int32),
            vmem((NZ, ROWS), f32),
            vmem((NZ, ROWS), f32),
            vmem((NZ, NZ, ROWS), f32),
            vmem((len(PLANE), 1, KEYS), f32),
            vmem((NX, NY, 1, KEYS), f32),
            vmem((NH, 2, 1, KEYS), f32),
            dma((4,)),
            dma((len(PLANE),)), dma((NX, NY)),
            dma((len(PLANE),)), dma((NX, NY)),
            dma((6 * PIECES + 2,)), dma((NZ, PIECES)),
            dma((NZ - 1,)), dma((NZ,)),
            dma((len(PLANE),)), dma((NX, NY)),
            dma((NH,)), dma((NH,)),
        ],
        compiler_params=pltpu.CompilerParams(
            collective_id=0, has_side_effects=True, vmem_limit_bytes=48 * 1024 * 1024
        ),
        name="key_scores",
    )(lengths, starts, queries, keys)


def solution(mesh):
    torus = Mesh(mesh.devices.reshape(NX, NZ, NY, NH), AXES)
    in_specs = (P(None, SEQ, "head"), P(None, SEQ, "head"), P(), P())
    out_specs = (P(None, "head", SEQ), P(None, SEQ))
    return jax.shard_map(body, mesh=torus, in_specs=in_specs, out_specs=out_specs, check_vma=False)
```

time: 205 us -> 59.2 us (0.29)
  blocking collectives: 110 us -> 0 us
  waiting for transfers between devices: 57.8 us -> 0 us
  Pallas kernels: 0 us -> 54.1 us
  between operations: 14.1 us -> 0.65 us
  other arithmetic: 12.5 us -> 0 us
  matrix products: 4.62 us -> 0 us
    all_gather x8 -> x0, blocking collectives: 83.7 us -> none  [the longest x6 66.9 us: merged_by_axis(): pieces = jax.tree.map(lambda part: lax.all_gather(part, axis), value)]
    all_gather x1 -> x0, waiting for transfers between devices: 57.7 us -> none  [all_blocks(): blocks = lax.all_gather(blocks, axes[k])]
    pallas_call x0 -> x1, Pallas kernels: none -> 54.1 us  [body(): pl.pallas_call(kernel, out_shape=(jax.ShapeDtypeStruct((2, KVH // NH, KEY...]
    psum x1 -> x0, blocking collectives: 26.3 us -> none  [body(): token_scores = lax.psum(jnp.sum(key_scores, axis=1), 'head')]
    reduce_sum x2 -> x0, other arithmetic: 10.5 us -> none  [the longest x1 6.44 us: body(): token_scores = lax.psum(jnp.sum(key_scores, axis=1), 'head')]
    dot_general x1 -> x0, matrix products: 4.62 us -> none  [body(): jnp.einsum('btghd,bkgd->bghtk', all_block, key_block, preferred_element_t...]
    transpose x2 -> x0, local copies, waits for them, and re-layouts: 3.07 us -> none  [the longest x1 2.49 us: all_blocks(): blocks = blocks.transpose(*back, *range(len(axes), blocks.ndim))]
    unnamed x1 -> x10, local copies, waits for them, and re-layouts: 1.41 us -> 4.26 us
  transfers between devices with their start and end apart: 1 -> 0, of which waited for: 1 -> 0; matrix products, arithmetic and copies ran while one was open for 1% -> 0% of each run, Pallas kernels for 0% -> 0%
where the time goes in v1:
time: 59.2 us; the launch traced here: 59 us
  Pallas kernels  54.1 us (91%)
  local copies, waits for them, and re-layouts  4.26 us (7%)
  between operations  0.65 us (1%)
    pallas_call x1, Pallas kernels, body(): pl.pallas_call(kernel, out_shape=(jax.ShapeDtypeStruct((2, KVH // NH, KEY...  54.1 us
    unnamed x10, local copies, waits for them, and re-layouts  4.26 us

profile of v1, /device:TPU:1, one launch (start us, length us, event | category | flops | bytes accessed | tf_op | source)
XLA Modules:
  0.0 59.0 jit_solution(13059499294385787290)
XLA Ops:
  0.6 0.0 copy-start
  0.6 0.9 %copy-done = bf16[2,256,256]{2,1,0:T(8,128)(2,1)S(1)} copy-done((bf16[2,256,256]{2,1,0:T(8,128)(2,1)S(1)}, bf16[2,256,256]{2,1,0:T(8,128)(2,1)}, u32[]{:S(2)}) %copy-start) | copy-done | bytes 262168
  1.6 0.0 copy-start.1
  1.6 0.8 %copy-done.1 = bf16[2,8,2048]{2,1,0:T(8,128)(2,1)S(1)} copy-done((bf16[2,8,2048]{2,1,0:T(8,128)(2,1)S(1)}, bf16[2,8,2048]{2,1,0:T(8,128)(2,1)}, u32[]{:S(2)}) %copy-start.1) | copy-done | bytes 65560
  2.4 0.0 copy-start.2
  2.4 0.7 %copy-done.2 = s32[2]{0:T(128)S(1)} copy-done((s32[2]{0:T(128)S(1)}, s32[2]{0:T(128)}, u32[]{:S(2)}) %copy-start.2) | copy-done | bytes 32
  3.1 0.0 copy-start.3
  3.1 0.7 %copy-done.3 = s32[2]{0:T(128)S(1)} copy-done((s32[2]{0:T(128)S(1)}, s32[2]{0:T(128)}, u32[]{:S(2)}) %copy-start.3) | copy-done | bytes 32
  3.7 54.1 %key_scores.1 = (f32[2,2,256]{2,1,0:T(2,128)S(1)}, f32[2,256]{1,0:T(2,128)S(1)}) custom-call(s32[2]{0:T(128)S(1)} %copy-done.2, s32[2]{0:T(128)S(1)} %copy-done.3, bf16[2,8,2048]{2,1,0:T(8,128)(2,1)S(1)} %copy-done.1, bf16[2,256,256]{2,1,0:T(8,128)(2,1)S(1)} %copy-done), custom_call_target="tpu_custom_call" | custom-call | tf_op jit(solution)/shard_map/key_scores/pallas_call | solution.py:251
  57.8 0.6 %copy.8 = f32[2,2,256]{2,1,0:T(2,128)} copy(f32[2,2,256]{2,1,0:T(2,128)S(1)} %get-tuple-element.4) | data formatting | bytes 8192
  58.4 0.6 copy.9
Async XLA Ops:
  0.6 1.0 %copy-start = (bf16[2,256,256]{2,1,0:T(8,128)(2,1)S(1)}, bf16[2,256,256]{2,1,0:T(8,128)(2,1)}, u32[]{:S(2)}) copy-start(bf16[2,256,256]{2,1,0:T(8,128)(2,1)} %k_hbm.1) | copy-start | bytes 786436
  1.6 0.8 %copy-start.1 = (bf16[2,8,2048]{2,1,0:T(8,128)(2,1)S(1)}, bf16[2,8,2048]{2,1,0:T(8,128)(2,1)}, u32[]{:S(2)}) copy-start(bf16[2,8,2048]{2,1,0:T(8,128)(2,1)} %q_hbm.1) | copy-start | bytes 196612
  2.4 0.7 %copy-start.2 = (s32[2]{0:T(128)S(1)}, s32[2]{0:T(128)}, u32[]{:S(2)}) copy-start(s32[2]{0:T(128)} %len_ref.1) | copy-start | bytes 28
  3.1 0.7 %copy-start.3 = (s32[2]{0:T(128)S(1)}, s32[2]{0:T(128)}, u32[]{:S(2)}) copy-start(s32[2]{0:T(128)} %start_ref.1) | copy-start | bytes 28

commit v2 on v1

v2 whole, which is shorter than its diff:
```python
import functools
import math

import jax
import jax.numpy as jnp
from jax import lax
from jax.experimental import pallas as pl
from jax.experimental.pallas import tpu as pltpu
from jax.sharding import Mesh
from jax.sharding import PartitionSpec as P

H = 64
KVH = 8
D = 128
QLEN = 512
SEQ = ("seq_0", "seq_1", "seq_2")
AXES = SEQ + ("head",)
NX, NZ, NY, NH = 4, 8, 2, 4
TOK = 8
KEYS = 256
HALF = H // KVH // NY
ROWS = NX * NY * TOK * HALF
BLOCKS = NX * NY
FILL = -1e30
SCALE2 = D**-0.5 * math.log2(math.e)
MESH = pl.DeviceIdType.MESH
PLANE = tuple((dx, dy) for dx in (2, 1, 3, 0) for dy in (1, 0) if (dx, dy) != (0, 0))
OFFSETS = (0, 1, -1, 2, -2, 3, -3, 4)
ARRIVAL = {off: j for j, off in enumerate(OFFSETS)}
PIECES = 2
PX = NX // PIECES
FORWARD_AT = 1


def wrap(value, size):
    return lax.rem(value + size, size)


def kernel(
    len_hbm, start_hbm, q_hbm, k_hbm, key_out, tok_out,
    len_ref, start_ref, qloc, kloc, qbuf, kbuf, sbuf, thr, msub, lsub, lse, accs, part, got,
    loc_sem, qs, qr, ks, kr, zs, zr, ss, sr, ps, pr,
):
    x, z, y, hd = (lax.axis_index(a) for a in AXES)
    f32, bf16 = jnp.float32, jnp.bfloat16

    def share_of(ref, px, py):
        b, g = px // 2, lax.rem(px, 2)
        lanes = pl.multiple_of(g * (NY * HALF * D) + py * (HALF * D), HALF * D)
        return ref.at[b, :, pl.ds(lanes, HALF * D)]

    def keys_of(ref, px):
        b, g = px // 2, lax.rem(px, 2)
        return ref.at[b, :, pl.ds(pl.multiple_of(g * D, D), D)]

    local = [
        pltpu.make_async_copy(q_hbm, qloc, loc_sem.at[0]),
        pltpu.make_async_copy(k_hbm, kloc, loc_sem.at[1]),
        pltpu.make_async_copy(share_of(q_hbm, x, y), qbuf.at[z, x, y], loc_sem.at[2]),
        pltpu.make_async_copy(keys_of(k_hbm, x), kbuf.at[x * NY + y], loc_sem.at[3]),
        pltpu.make_async_copy(len_hbm, len_ref, loc_sem.at[4]),
        pltpu.make_async_copy(start_hbm, start_ref, loc_sem.at[5]),
    ]
    for copy in local:
        copy.start()

    barrier = pltpu.get_barrier_semaphore()
    partners = [(x, wrap(z + dz, NZ), y, hd) for dz in (2, -2, 1, -1)]
    partners += [
        (wrap(x + dx, NX), z, wrap(y + dy, NY), wrap(hd + dh, NH))
        for dx, dy in PLANE + ((0, 0),) for dh in range(NH) if (dx, dy, dh) != (0, 0, 0)
    ]
    for partner in partners:
        pl.semaphore_signal(barrier, inc=1, device_id=partner, device_id_type=MESH)
    for copy in local:
        copy.wait()
    pl.semaphore_wait(barrier, len(partners))

    def remote(src, dst, send, recv, device):
        return pltpu.make_async_remote_copy(
            src_ref=src, dst_ref=dst, send_sem=send, recv_sem=recv,
            device_id=device, device_id_type=MESH,
        )

    started = []

    def start(copy):
        copy.start()
        started.append(copy)

    for n, (dx, dy) in enumerate(PLANE):
        px, py = wrap(x + dx, NX), wrap(y + dy, NY)
        start(remote(share_of(qloc, px, py), qbuf.at[z, x, y], qs.at[n], qr.at[x, y], (px, z, py, hd)))
    for n, (dx, dy) in enumerate(PLANE):
        px, py = wrap(x + dx, NX), wrap(y + dy, NY)
        start(remote(keys_of(kloc, px), kbuf.at[x * NY + y], ks.at[n], kr.at[x, y], (px, z, py, hd)))

    b = x // 2
    start_pos = start_ref[b]
    first_pos = len_ref[b] - QLEN
    for px in range(NX):
        for py in range(NY):
            pos = ((px * NZ + z) * NY + py) * KEYS + lax.broadcasted_iota(jnp.int32, (KEYS, D), 0)
            thr[px * NY + py] = jnp.where(pos >= start_pos, pos, jnp.int32(2**30))

    def z_copy(off, piece, dz, n):
        slot = wrap(z + off, NZ)
        rows = pl.ds(piece * PX, PX)
        there = off - dz
        j = ARRIVAL[there] if there in ARRIVAL else ARRIVAL[-there]
        return remote(
            qbuf.at[slot, rows], qbuf.at[slot, rows], zs.at[n], zr.at[j, piece],
            (x, wrap(z + dz, NZ), y, hd),
        )

    def z_wait(off, piece):
        slot = wrap(z + off, NZ)
        rows = pl.ds(piece * PX, PX)
        remote(
            qbuf.at[slot, rows], qbuf.at[slot, rows], zs.at[0], zr.at[ARRIVAL[off], piece],
            (x, wrap(z + 1, NZ), y, hd),
        ).wait_recv()

    sends = [0]

    def z_start(off, piece, dz):
        start(z_copy(off, piece, dz, sends[0]))
        sends[0] += 1

    def z_forward(hop):
        for piece in range(PIECES):
            for side in (1, -1):
                z_wait(side * hop, piece)
                z_start(side * hop, piece, -side)
                if hop == 2 and piece == (0 if side == -1 else PIECES - 1):
                    z_start(side * hop, piece, -2 * side)

    for dx, dy in PLANE[::-1]:
        px, py = wrap(x + dx, NX), wrap(y + dy, NY)
        remote(
            share_of(qloc, px, py), qbuf.at[z, px, py], qs.at[0], qr.at[px, py], (px, z, py, hd)
        ).wait_recv()
    for piece in range(PIECES):
        for dz in (1, -1):
            z_start(0, piece, dz)
    z_forward(1)

    def rows_of(c):
        wide = qbuf[c].astype(f32).reshape(BLOCKS * TOK, HALF * D)
        q = jnp.concatenate([wide[:, h * D:(h + 1) * D] for h in range(HALF)], axis=0).astype(bf16)
        lane = lax.rem(lax.broadcasted_iota(jnp.int32, (1, ROWS), 1), BLOCKS * TOK)
        inner = NY * TOK
        return q, first_pos + (lane // inner) * (NZ * inner) + c * inner + lax.rem(lane, inner)

    def score(c, q, query_pos, n):
        s = lax.dot_general(kbuf[n], q, (((1,), (1,)), ((), ())), preferred_element_type=f32)
        limit = thr[n]
        s = jnp.where(jnp.concatenate([limit, limit], axis=1) <= query_pos, s, FILL)
        top = jnp.max(s, axis=0, keepdims=True)
        e = jnp.exp2((s - top) * SCALE2)
        sbuf[c, n] = e
        msub[c, pl.ds(n, 1), :] = top
        lsub[c, pl.ds(n, 1), :] = jnp.sum(e, axis=0, keepdims=True)

    def merge(c):
        tops = msub[c] * SCALE2
        top = jnp.max(tops, axis=0, keepdims=True)
        total = jnp.sum(lsub[c] * jnp.exp2(tops - top), axis=0, keepdims=True)
        lse[z, pl.ds(c, 1), :] = top + jnp.log2(total)

    q, query_pos = rows_of(z)
    score(z, q, query_pos, x * NY + y)
    for dx, dy in PLANE[::-1]:
        px, py = wrap(x + dx, NX), wrap(y + dy, NY)
        remote(
            keys_of(kloc, px), kbuf.at[px * NY + py], ks.at[0], kr.at[px, py], (px, z, py, hd)
        ).wait_recv()
        score(z, q, query_pos, px * NY + py)
    merge(z)
    for j, off in enumerate(OFFSETS):
        if off == 0:
            continue
        if off == FORWARD_AT:
            z_forward(2)
        if abs(off) > 2:
            for piece in range(PIECES):
                z_wait(off, piece)
        c = wrap(z + off, NZ)
        q, query_pos = rows_of(c)
        for n in range(BLOCKS):
            score(c, q, query_pos, n)
        merge(c)

    for n, dz in enumerate((4, 3, -3, 2, -2, 1, -1)):
        start(remote(lse.at[z], lse.at[z], ss.at[n], sr.at[z], (x, wrap(z + dz, NZ), y, hd)))
    for dz in (1, -1, 2, -2, 3, -3, 4):
        other = wrap(z + dz, NZ)
        remote(lse.at[other], lse.at[other], ss.at[0], sr.at[other], (x, other, y, hd)).wait_recv()
    every = [lse[k] for k in range(NZ)]
    peak = functools.reduce(jnp.maximum, every)
    whole = peak + jnp.log2(sum(jnp.exp2(v - peak) for v in every))
    for c in range(NZ):
        msub[c] = jnp.exp2(msub[c] * SCALE2 - whole[c:c + 1])

    def weigh(n, carry):
        for half in range(2):
            rows = pl.ds(half * D, D)
            acc = jnp.zeros((D, D), f32)
            for c in range(NZ):
                w = msub[c, pl.ds(n, 1), :]
                acc = acc + sbuf[c, n, rows, :D] * w[:, :D]
                acc = acc + sbuf[c, n, rows, D:] * w[:, D:]
            accs[n, rows] = acc
        return carry

    lax.fori_loop(0, BLOCKS, weigh, 0)
    ones = jnp.ones((16, D), bf16)
    for n in range(BLOCKS):
        acc = accs[n]
        hi = acc.astype(bf16)
        rest = acc - hi.astype(f32)
        mid = rest.astype(bf16)
        low = (rest - mid.astype(f32)).astype(bf16)
        sums = sum(
            lax.dot_general(ones, v, (((1,), (1,)), ((), ())), preferred_element_type=f32)
            for v in (low, mid, hi)
        )
        part[n] = sums[0:1]
    got[hd, x, y] = part[x * NY + y]
    owners = [
        (dx, dy, dh) for dx, dy in PLANE + ((0, 0),) for dh in range(NH) if (dx, dy, dh) != (0, 0, 0)
    ]
    for n, (dx, dy, dh) in enumerate(owners):
        px, py, ph = wrap(x + dx, NX), wrap(y + dy, NY), wrap(hd + dh, NH)
        start(remote(
            part.at[px * NY + py], got.at[hd, x, y], ps.at[n], pr.at[hd, x, y], (px, z, py, ph)
        ))
    for n, (dx, dy, dh) in enumerate(owners[::-1]):
        px, py, ph = wrap(x + dx, NX), wrap(y + dy, NY), wrap(hd + dh, NH)
        remote(
            part.at[px * NY + py], got.at[ph, px, py], ps.at[n], pr.at[ph, px, py], (px, z, py, ph)
        ).wait_recv()

    heads = KVH // NH
    for request in range(2):
        total = None
        for k in range(NH):
            for g in range(heads):
                pair = request * heads + g
                sums = got[k, pair, 0] + got[k, pair, 1]
                total = sums if total is None else total + sums
        tok_out[request:request + 1] = total
        for g in range(heads):
            pair = request * heads + g
            key_out[request, g:g + 1] = got[hd, pair, 0] + got[hd, pair, 1]

    for copy in started:
        copy.wait_send()


def body(queries, keys, lengths, starts):
    f32, bf16 = jnp.float32, jnp.bfloat16
    dma = pltpu.SemaphoreType.DMA
    vmem = pltpu.VMEM
    return pl.pallas_call(
        kernel,
        out_shape=(
            jax.ShapeDtypeStruct((2, KVH // NH, KEYS), f32),
            jax.ShapeDtypeStruct((2, KEYS), f32),
        ),
        in_specs=[pl.BlockSpec(memory_space=pltpu.HBM)] * 4,
        out_specs=(pl.BlockSpec(memory_space=vmem), pl.BlockSpec(memory_space=vmem)),
        scratch_shapes=[
            pltpu.SMEM((2,), jnp.int32),
            pltpu.SMEM((2,), jnp.int32),
            vmem(queries.shape, bf16),
            vmem(keys.shape, bf16),
            vmem((NZ, NX, NY, TOK, HALF * D), bf16),
            vmem((BLOCKS, KEYS, D), bf16),
            vmem((NZ, BLOCKS, KEYS, ROWS), f32),
            vmem((BLOCKS, KEYS, D), jnp.int32),
            vmem((NZ, BLOCKS, ROWS), f32),
            vmem((NZ, BLOCKS, ROWS), f32),
            vmem((NZ, NZ, ROWS), f32),
            vmem((BLOCKS, KEYS, D), f32),
            vmem((BLOCKS, 1, KEYS), f32),
            vmem((NH, NX, NY, 1, KEYS), f32),
            dma((6,)),
            dma((len(PLANE),)), dma((NX, NY)),
            dma((len(PLANE),)), dma((NX, NY)),
            dma((6 * PIECES + 2,)), dma((NZ, PIECES)),
            dma((NZ - 1,)), dma((NZ,)),
            dma((NH * BLOCKS - 1,)), dma((NH, NX, NY)),
        ],
        compiler_params=pltpu.CompilerParams(
            collective_id=0, has_side_effects=True, vmem_limit_bytes=67043328
        ),
        name="key_scores",
    )(lengths, starts, queries, keys)


def solution(mesh):
    torus = Mesh(mesh.devices.reshape(NX, NZ, NY, NH), AXES)
    in_specs = (P(None, SEQ, "head"), P(None, SEQ, "head"), P(), P())
    out_specs = (P(None, "head", SEQ), P(None, SEQ))
    return jax.shard_map(body, mesh=torus, in_specs=in_specs, out_specs=out_specs, check_vma=False)
```

time: 59.2 us -> 45.3 us (0.77)
  Pallas kernels: 54.1 us -> 42.6 us
  local copies, waits for them, and re-layouts: 4.26 us -> 1.85 us
    pallas_call x1, Pallas kernels: 54.1 us -> 42.6 us  [body(): pl.pallas_call(kernel, out_shape=(jax.ShapeDtypeStruct((2, KVH // NH, KEY...]
    unnamed x10 -> x4, local copies, waits for them, and re-layouts: 4.26 us -> 1.85 us
where the time goes in v2:
time: 45.3 us; the launch traced here: 45.1 us
  Pallas kernels  42.6 us (94%)
  local copies, waits for them, and re-layouts  1.85 us (4%)
  between operations  0.65 us (1%)
    pallas_call x1, Pallas kernels, body(): pl.pallas_call(kernel, out_shape=(jax.ShapeDtypeStruct((2, KVH // NH, KEY...  42.6 us
    unnamed x4, local copies, waits for them, and re-layouts  1.85 us

profile of v2, /device:TPU:1, one launch (start us, length us, event | category | flops | bytes accessed | tf_op | source)
XLA Modules:
  0.0 45.1 jit_solution(7865467693624520540)
XLA Ops:
  0.6 42.6 %key_scores.1 = (f32[2,2,256]{2,1,0:T(2,128)}, f32[2,256]{1,0:T(2,128)}) custom-call(s32[2]{0:T(128)} %len_hbm.1, s32[2]{0:T(128)} %start_hbm.1, bf16[2,8,2048]{2,1,0:T(8,128)(2,1)} %q_hbm.1, bf16[2,256,256]{2,1,0:T(8,128)(2,1)} %k_hbm.1), custom_call_target="tpu_custom_call" | custom-call | tf_op jit(solution)/shard_map/key_scores/pallas_call | solution.py:265
  43.3 0.0 copy-start
  43.3 1.3 %copy.8 = f32[2,2,256]{2,1,0:T(2,128)} copy(f32[2,2,256]{2,1,0:T(2,128)} %get-tuple-element.4) | data formatting | bytes 8192
  44.6 0.0 copy-done
  44.6 0.6 %copy.9 = f32[2,256]{1,0:T(2,128)} copy(f32[2,256]{1,0:T(2,128)S(1)} %copy-done) | data formatting | bytes 4096
Async XLA Ops:
  43.3 1.3 %copy-start = (f32[2,256]{1,0:T(2,128)S(1)}, f32[2,256]{1,0:T(2,128)}, u32[]{:S(2)}) copy-start(f32[2,256]{1,0:T(2,128)} %get-tuple-element.5) | copy-start | bytes 6148

commit v3 on v2

v3 whole, which is shorter than its diff:
```python
import functools
import math

import jax
import jax.numpy as jnp
from jax import lax
from jax.experimental import pallas as pl
from jax.experimental.pallas import tpu as pltpu
from jax.sharding import Mesh
from jax.sharding import PartitionSpec as P

H = 64
KVH = 8
D = 128
QLEN = 512
SEQ = ("seq_0", "seq_1", "seq_2")
AXES = SEQ + ("head",)
NX, NZ, NY, NH = 4, 8, 2, 4
TOK = 8
KEYS = 256
HALF = H // KVH // NY
ROWS = NX * NY * TOK * HALF
BLOCKS = NX * NY
FILL = -1e30
SCALE2 = D**-0.5 * math.log2(math.e)
MESH = pl.DeviceIdType.MESH
PLANE = tuple((dx, dy) for dx in (2, 1, 3, 0) for dy in (1, 0) if (dx, dy) != (0, 0))
OFFSETS = (0, 1, -1, 2, -2, 3, -3, 4)
ARRIVAL = {off: j for j, off in enumerate(OFFSETS)}
STRIDES = (0, 1, 3, 2)
NEAR = (0, 1, -1)
FORWARD_AT = 5


def wrap(value, size):
    return lax.rem(value + size, size)


def kernel(
    len_hbm, start_hbm, q_hbm, k_hbm, key_out, tok_out,
    len_ref, start_ref, qloc, kloc, qbuf, kbuf, sbuf, thr, msub, lsub, lse, part, got,
    loc_sem, qs, qr, ks, kr, zs, zr, ss, sr, ps, pr,
):
    x, z, y, hd = (lax.axis_index(a) for a in AXES)
    f32, bf16 = jnp.float32, jnp.bfloat16

    def share_of(ref, px, py):
        b, g = px // 2, lax.rem(px, 2)
        lanes = pl.multiple_of(g * (NY * HALF * D) + py * (HALF * D), HALF * D)
        return ref.at[b, :, pl.ds(lanes, HALF * D)]

    def keys_of(ref, px):
        b, g = px // 2, lax.rem(px, 2)
        return ref.at[b, :, pl.ds(pl.multiple_of(g * D, D), D)]

    local = [
        pltpu.make_async_copy(q_hbm, qloc, loc_sem.at[0]),
        pltpu.make_async_copy(k_hbm, kloc, loc_sem.at[1]),
        pltpu.make_async_copy(share_of(q_hbm, x, y), qbuf.at[z, x, y], loc_sem.at[2]),
        pltpu.make_async_copy(keys_of(k_hbm, x), kbuf.at[x * NY + y], loc_sem.at[3]),
        pltpu.make_async_copy(len_hbm, len_ref, loc_sem.at[4]),
        pltpu.make_async_copy(start_hbm, start_ref, loc_sem.at[5]),
    ]
    for copy in local:
        copy.start()

    barrier = pltpu.get_barrier_semaphore()
    everywhere = PLANE + ((0, 0),)
    partners = [(x, wrap(z + dz, NZ), y, hd) for dz in (2, -2)]
    partners += [
        (wrap(x + dx, NX), wrap(z + dz, NZ), wrap(y + dy, NY), hd)
        for dz in (1, -1) for dx, dy in everywhere
    ]
    partners += [
        (wrap(x + dx, NX), z, wrap(y + dy, NY), wrap(hd + dh, NH))
        for dx, dy in everywhere for dh in range(NH) if (dx, dy, dh) != (0, 0, 0)
    ]
    for partner in partners:
        pl.semaphore_signal(barrier, inc=1, device_id=partner, device_id_type=MESH)
    for copy in local:
        copy.wait()
    pl.semaphore_wait(barrier, len(partners))

    def remote(src, dst, send, recv, device):
        return pltpu.make_async_remote_copy(
            src_ref=src, dst_ref=dst, send_sem=send, recv_sem=recv,
            device_id=device, device_id_type=MESH,
        )

    started = []

    def start(copy, apart=True):
        copy.start()
        if apart:
            started.append(copy)

    sends = [0]
    for dz in NEAR:
        for dx, dy in PLANE if dz == 0 else everywhere:
            px, py = wrap(x + dx, NX), wrap(y + dy, NY)
            start(remote(
                share_of(qloc, px, py), qbuf.at[z, x, y], qs.at[sends[0]], qr.at[ARRIVAL[-dz], x, y],
                (px, wrap(z + dz, NZ), py, hd),
            ))
            sends[0] += 1

    def q_wait(off, dx):
        for dy in (0, 1):
            if (off, dx, dy) != (0, 0, 0):
                px, py, pz = wrap(x + dx, NX), wrap(y + dy, NY), wrap(z + off, NZ)
                remote(
                    share_of(qloc, px, py), qbuf.at[pz, px, py], qs.at[0], qr.at[ARRIVAL[off], px, py],
                    (px, wrap(z + 1, NZ), py, hd),
                ).wait_recv()

    for n, (dx, dy) in enumerate(PLANE):
        px, py = wrap(x + dx, NX), wrap(y + dy, NY)
        start(remote(keys_of(kloc, px), kbuf.at[x * NY + y], ks.at[n], kr.at[x, y], (px, z, py, hd)))

    b = x // 2
    start_pos = start_ref[b]
    first_pos = len_ref[b] - QLEN
    for px in range(NX):
        for py in range(NY):
            pos = ((px * NZ + z) * NY + py) * KEYS + lax.broadcasted_iota(jnp.int32, (KEYS, D), 0)
            thr[px * NY + py] = jnp.where(pos >= start_pos, pos, jnp.int32(2**30))

    def z_copy(off, i, dz, n):
        slot, px = wrap(z + off, NZ), wrap(x + STRIDES[i], NX)
        there = off - dz
        j = ARRIVAL[there] if there in ARRIVAL else ARRIVAL[-there]
        return remote(
            qbuf.at[slot, px], qbuf.at[slot, px], zs.at[n], zr.at[j, i], (x, wrap(z + dz, NZ), y, hd)
        )

    def z_wait(off, i):
        slot, px = wrap(z + off, NZ), wrap(x + STRIDES[i], NX)
        remote(
            qbuf.at[slot, px], qbuf.at[slot, px], zs.at[0], zr.at[ARRIVAL[off], i],
            (x, wrap(z + 1, NZ), y, hd),
        ).wait_recv()

    sends = [0]

    def z_start(off, i, dz):
        start(z_copy(off, i, dz, sends[0]))
        sends[0] += 1

    def z_forward(i):
        for side in (1, -1):
            z_wait(side * 2, i)
            if (i % 2 == 0) == (side == 1):
                z_start(side * 2, i, -2 * side)
            z_start(side * 2, i, -side)

    for i, dx in enumerate(STRIDES):
        for side in (1, -1):
            q_wait(side, dx)
            z_start(side, i, -side)
    for dx in STRIDES:
        q_wait(0, dx)

    def rows_of(c):
        wide = qbuf[c].astype(f32).reshape(BLOCKS * TOK, HALF * D)
        q = jnp.concatenate([wide[:, h * D:(h + 1) * D] for h in range(HALF)], axis=0).astype(bf16)
        lane = lax.rem(lax.broadcasted_iota(jnp.int32, (1, ROWS), 1), BLOCKS * TOK)
        inner = NY * TOK
        return q, first_pos + (lane // inner) * (NZ * inner) + c * inner + lax.rem(lane, inner)

    def score(c, q, query_pos, n):
        s = lax.dot_general(kbuf[n], q, (((1,), (1,)), ((), ())), preferred_element_type=f32)
        limit = thr[n]
        s = jnp.where(jnp.concatenate([limit, limit], axis=1) <= query_pos, s, FILL)
        top = jnp.max(s, axis=0, keepdims=True)
        e = jnp.exp2((s - top) * SCALE2)
        sbuf[c, n] = e
        msub[c, pl.ds(n, 1), :] = top
        lsub[c, pl.ds(n, 1), :] = jnp.sum(e, axis=0, keepdims=True)

    def merge(c):
        tops = msub[c] * SCALE2
        top = jnp.max(tops, axis=0, keepdims=True)
        total = jnp.sum(lsub[c] * jnp.exp2(tops - top), axis=0, keepdims=True)
        lse[z, pl.ds(c, 1), :] = top + jnp.log2(total)

    near = [(wrap(z + off, NZ),) + rows_of(wrap(z + off, NZ)) for off in NEAR]
    for n, (dx, dy) in enumerate(((0, 0),) + PLANE):
        px, py = wrap(x + dx, NX), wrap(y + dy, NY)
        if n > 0:
            remote(
                keys_of(kloc, px), kbuf.at[px * NY + py], ks.at[0], kr.at[px, py], (px, z, py, hd)
            ).wait_recv()
        for c, q, query_pos in near:
            score(c, q, query_pos, px * NY + py)
        if n == FORWARD_AT:
            for i in range(NX):
                z_forward(i)
    for offs in ((2, -2), (3, -3), (4,)):
        for off in offs:
            if abs(off) > 2:
                for i in range(NX):
                    z_wait(off, i)
        far = [(wrap(z + off, NZ),) + rows_of(wrap(z + off, NZ)) for off in offs]
        for c, q, query_pos in far:
            for n in range(BLOCKS):
                score(c, q, query_pos, n)
        if offs == (2, -2):
            for off in NEAR:
                merge(wrap(z + off, NZ))
        for off in offs:
            merge(wrap(z + off, NZ))

    for dz in (4, 3, -3, 2, -2, 1, -1):
        start(remote(lse.at[z], lse.at[z], ss.at[0], sr.at[0], (x, wrap(z + dz, NZ), y, hd)), False)
    others = lse.at[pl.ds(0, NZ - 1)]
    stats = remote(others, others, ss.at[0], sr.at[0], (x, wrap(z + 1, NZ), y, hd))
    stats.wait_recv()
    every = [lse[k] for k in range(NZ)]
    peak = functools.reduce(jnp.maximum, every)
    whole = peak + jnp.log2(sum(jnp.exp2(v - peak) for v in every))
    for c in range(NZ):
        msub[c] = jnp.exp2(msub[c] * SCALE2 - whole[c:c + 1])

    ones = jnp.ones((16, 2 * D), bf16)

    def weigh(n):
        parts = []
        for half in range(2):
            rows = pl.ds(half * D, D)
            acc = jnp.zeros((D, D), f32)
            for c in range(NZ):
                w = msub[c, pl.ds(n, 1), :]
                acc = acc + sbuf[c, n, rows, :D] * w[:, :D]
                acc = acc + sbuf[c, n, rows, D:] * w[:, D:]
            high = acc.astype(bf16)
            low = (acc - high.astype(f32)).astype(bf16)
            parts.append(jnp.concatenate([high, low], axis=1))
        return lax.dot_general(
            ones, jnp.concatenate(parts, axis=0), (((1,), (1,)), ((), ())), preferred_element_type=f32
        )[0:1]

    def send_sums(dx, dy, sums):
        px, py = wrap(x + dx, NX), wrap(y + dy, NY)
        if (dx, dy) == (0, 0):
            got[hd, x, y] = sums
        part[px * NY + py] = sums
        for dh in (2, 3, 1, 0):
            if (dx, dy, dh) != (0, 0, 0):
                start(remote(
                    part.at[px * NY + py], got.at[hd, x, y], ps.at[0], pr.at[0],
                    (px, z, py, wrap(hd + dh, NH)),
                ), False)

    held = None
    for dx, dy in everywhere:
        sums = weigh(wrap(x + dx, NX) * NY + wrap(y + dy, NY))
        if held is not None:
            send_sums(*held)
        held = (dx, dy, sums)
    send_sums(*held)
    every_sum = got.reshape(NH * BLOCKS, 1, KEYS).at[pl.ds(0, NH * BLOCKS - 1)]
    returned = remote(every_sum, every_sum, ps.at[0], pr.at[0], (x, wrap(z + 1, NZ), y, hd))
    returned.wait_recv()

    heads = KVH // NH
    for request in range(2):
        total = None
        for k in range(NH):
            for g in range(heads):
                pair = request * heads + g
                sums = got[k, pair, 0] + got[k, pair, 1]
                total = sums if total is None else total + sums
        tok_out[request:request + 1] = total
        for g in range(heads):
            pair = request * heads + g
            key_out[request, g:g + 1] = got[hd, pair, 0] + got[hd, pair, 1]

    for copy in started + [stats, returned]:
        copy.wait_send()


def body(queries, keys, lengths, starts):
    f32, bf16 = jnp.float32, jnp.bfloat16
    dma = pltpu.SemaphoreType.DMA
    vmem = pltpu.VMEM
    return pl.pallas_call(
        kernel,
        out_shape=(
            jax.ShapeDtypeStruct((2, KVH // NH, KEYS), f32),
            jax.ShapeDtypeStruct((2, KEYS), f32),
        ),
        in_specs=[pl.BlockSpec(memory_space=pltpu.HBM)] * 4,
        out_specs=(pl.BlockSpec(memory_space=vmem), pl.BlockSpec(memory_space=vmem)),
        scratch_shapes=[
            pltpu.SMEM((2,), jnp.int32),
            pltpu.SMEM((2,), jnp.int32),
            vmem(queries.shape, bf16),
            vmem(keys.shape, bf16),
            vmem((NZ, NX, NY, TOK, HALF * D), bf16),
            vmem((BLOCKS, KEYS, D), bf16),
            vmem((NZ, BLOCKS, KEYS, ROWS), f32),
            vmem((BLOCKS, KEYS, D), jnp.int32),
            vmem((NZ, BLOCKS, ROWS), f32),
            vmem((NZ, BLOCKS, ROWS), f32),
            vmem((NZ, NZ, ROWS), f32),
            vmem((BLOCKS, 1, KEYS), f32),
            vmem((NH, NX, NY, 1, KEYS), f32),
            dma((6,)),
            dma((3 * BLOCKS - 1,)), dma((3, NX, NY)),
            dma((len(PLANE),)), dma((NX, NY)),
            dma((5 * NX,)), dma((NZ, NX)),
            dma((1,)), dma((1,)),
            dma((1,)), dma((1,)),
        ],
        compiler_params=pltpu.CompilerParams(
            collective_id=0, has_side_effects=True, vmem_limit_bytes=67043328
        ),
        name="key_scores",
    )(lengths, starts, queries, keys)


def solution(mesh):
    torus = Mesh(mesh.devices.reshape(NX, NZ, NY, NH), AXES)
    in_specs = (P(None, SEQ, "head"), P(None, SEQ, "head"), P(), P())
    out_specs = (P(None, "head", SEQ), P(None, SEQ))
    return jax.shard_map(body, mesh=torus, in_specs=in_specs, out_specs=out_specs, check_vma=False)
```

time: 45.3 us -> 43.3 us (0.956)
  Pallas kernels: 42.6 us -> 40.6 us
    pallas_call x1, Pallas kernels: 42.6 us -> 40.6 us  [body(): pl.pallas_call(kernel, out_shape=(jax.ShapeDtypeStruct((2, KVH // NH, KEY...]
where the time goes in v3:
time: 43.3 us; the launch traced here: 43.1 us
  Pallas kernels  40.6 us (94%)
  local copies, waits for them, and re-layouts  1.85 us (4%)
  between operations  0.65 us (2%)
    pallas_call x1, Pallas kernels, body(): pl.pallas_call(kernel, out_shape=(jax.ShapeDtypeStruct((2, KVH // NH, KEY...  40.6 us
    unnamed x4, local copies, waits for them, and re-layouts  1.85 us

profile of v3, /device:TPU:1, one launch (start us, length us, event | category | flops | bytes accessed | tf_op | source)
XLA Modules:
  0.0 43.1 jit_solution(805582036845543802)
XLA Ops:
  0.6 40.6 %key_scores.1 = (f32[2,2,256]{2,1,0:T(2,128)}, f32[2,256]{1,0:T(2,128)}) custom-call(s32[2]{0:T(128)} %len_hbm.1, s32[2]{0:T(128)} %start_hbm.1, bf16[2,8,2048]{2,1,0:T(8,128)(2,1)} %q_hbm.1, bf16[2,256,256]{2,1,0:T(8,128)(2,1)} %k_hbm.1), custom_call_target="tpu_custom_call" | custom-call | tf_op jit(solution)/shard_map/key_scores/pallas_call | solution.py:286
  41.3 0.0 copy-start
  41.3 1.3 %copy.8 = f32[2,2,256]{2,1,0:T(2,128)} copy(f32[2,2,256]{2,1,0:T(2,128)} %get-tuple-element.4) | data formatting | bytes 8192
  42.5 0.0 copy-done
  42.6 0.6 %copy.9 = f32[2,256]{1,0:T(2,128)} copy(f32[2,256]{1,0:T(2,128)S(1)} %copy-done) | data formatting | bytes 4096
Async XLA Ops:
  41.3 1.3 %copy-start = (f32[2,256]{1,0:T(2,128)S(1)}, f32[2,256]{1,0:T(2,128)}, u32[]{:S(2)}) copy-start(f32[2,256]{1,0:T(2,128)} %get-tuple-element.5) | copy-start | bytes 6148

commit v4 on v3

--- a/solution.py
+++ b/solution.py
@@ -29,7 +29,9 @@
 ARRIVAL = {off: j for j, off in enumerate(OFFSETS)}
 STRIDES = (0, 1, 3, 2)
 NEAR = (0, 1, -1)
-FORWARD_AT = 5
+FORWARD_AT = (2, 2, 2, 2)
+KEY_ORDER = ((0, 1), (3, 0), (1, 0), (3, 1), (1, 1), (2, 0), (2, 1))
+FIRST_KEYS = KEY_ORDER[:3]
 
 
 def wrap(value, size):
@@ -39,7 +41,7 @@
 def kernel(
     len_hbm, start_hbm, q_hbm, k_hbm, key_out, tok_out,
     len_ref, start_ref, qloc, kloc, qbuf, kbuf, sbuf, thr, msub, lsub, lse, part, got,
-    loc_sem, qs, qr, ks, kr, zs, zr, ss, sr, ps, pr,
+    loc_sem, ready, qs, qr, ks, kr, zs, zr, ss, sr, ps, pr,
 ):
     x, z, y, hd = (lax.axis_index(a) for a in AXES)
     f32, bf16 = jnp.float32, jnp.bfloat16
@@ -66,20 +68,17 @@
 
     barrier = pltpu.get_barrier_semaphore()
     everywhere = PLANE + ((0, 0),)
-    partners = [(x, wrap(z + dz, NZ), y, hd) for dz in (2, -2)]
-    partners += [
-        (wrap(x + dx, NX), wrap(z + dz, NZ), wrap(y + dy, NY), hd)
-        for dz in (1, -1) for dx, dy in everywhere
-    ]
-    partners += [
-        (wrap(x + dx, NX), z, wrap(y + dy, NY), wrap(hd + dh, NH))
-        for dx, dy in everywhere for dh in range(NH) if (dx, dy, dh) != (0, 0, 0)
-    ]
+    beside = [(x, wrap(z + dz, NZ), y, hd) for dz in (1, -1)]
+    heads_here = [(x, z, y, wrap(hd + dh, NH)) for dh in range(1, NH)]
+    partners = beside + [(wrap(x + dx, NX), z, wrap(y + dy, NY), hd) for dx, dy in PLANE] + heads_here
     for partner in partners:
         pl.semaphore_signal(barrier, inc=1, device_id=partner, device_id_type=MESH)
-    for copy in local:
-        copy.wait()
+    local[0].wait()
     pl.semaphore_wait(barrier, len(partners))
+    for partner in beside:
+        pl.semaphore_signal(ready.at[0], inc=1, device_id=partner, device_id_type=MESH)
+    for partner in heads_here:
+        pl.semaphore_signal(ready.at[1], inc=1, device_id=partner, device_id_type=MESH)
 
     def remote(src, dst, send, recv, device):
         return pltpu.make_async_remote_copy(
@@ -95,14 +94,35 @@
             started.append(copy)
 
     sends = [0]
-    for dz in NEAR:
-        for dx, dy in PLANE if dz == 0 else everywhere:
-            px, py = wrap(x + dx, NX), wrap(y + dy, NY)
-            start(remote(
-                share_of(qloc, px, py), qbuf.at[z, x, y], qs.at[sends[0]], qr.at[ARRIVAL[-dz], x, y],
-                (px, wrap(z + dz, NZ), py, hd),
-            ))
-            sends[0] += 1
+
+    def q_start(dz, dx, dy):
+        px, py = wrap(x + dx, NX), wrap(y + dy, NY)
+        start(remote(
+            share_of(qloc, px, py), qbuf.at[z, x, y], qs.at[sends[0]], qr.at[ARRIVAL[-dz], x, y],
+            (px, wrap(z + dz, NZ), py, hd),
+        ))
+        sends[0] += 1
+
+    def k_start(dx, dy):
+        px, py = wrap(x + dx, NX), wrap(y + dy, NY)
+        n = PLANE.index((dx, dy))
+        start(remote(keys_of(kloc, px), kbuf.at[x * NY + y], ks.at[n], kr.at[x, y], (px, z, py, hd)))
+
+    for dx, dy in PLANE:
+        q_start(0, dx, dy)
+    for dz in (1, -1):
+        q_start(dz, 0, 0)
+    for copy in local[1:]:
+        copy.wait()
+    for dx, dy in FIRST_KEYS:
+        k_start(dx, dy)
+    pl.semaphore_wait(ready.at[0], len(beside))
+    for dx, dy in PLANE:
+        for dz in (1, -1):
+            q_start(dz, dx, dy)
+    for dx, dy in KEY_ORDER:
+        if (dx, dy) not in FIRST_KEYS:
+            k_start(dx, dy)
 
     def q_wait(off, dx):
         for dy in (0, 1):
@@ -112,10 +132,6 @@
                     share_of(qloc, px, py), qbuf.at[pz, px, py], qs.at[0], qr.at[ARRIVAL[off], px, py],
                     (px, wrap(z + 1, NZ), py, hd),
                 ).wait_recv()
-
-    for n, (dx, dy) in enumerate(PLANE):
-        px, py = wrap(x + dx, NX), wrap(y + dy, NY)
-        start(remote(keys_of(kloc, px), kbuf.at[x * NY + y], ks.at[n], kr.at[x, y], (px, z, py, hd)))
 
     b = x // 2
     start_pos = start_ref[b]
@@ -184,7 +200,7 @@
         lse[z, pl.ds(c, 1), :] = top + jnp.log2(total)
 
     near = [(wrap(z + off, NZ),) + rows_of(wrap(z + off, NZ)) for off in NEAR]
-    for n, (dx, dy) in enumerate(((0, 0),) + PLANE):
+    for n, (dx, dy) in enumerate(((0, 0),) + KEY_ORDER):
         px, py = wrap(x + dx, NX), wrap(y + dy, NY)
         if n > 0:
             remote(
@@ -192,8 +208,8 @@
             ).wait_recv()
         for c, q, query_pos in near:
             score(c, q, query_pos, px * NY + py)
-        if n == FORWARD_AT:
-            for i in range(NX):
+        for i in range(NX):
+            if n == FORWARD_AT[i]:
                 z_forward(i)
     for offs in ((2, -2), (3, -3), (4,)):
         for off in offs:
@@ -214,6 +230,10 @@
         start(remote(lse.at[z], lse.at[z], ss.at[0], sr.at[0], (x, wrap(z + dz, NZ), y, hd)), False)
     others = lse.at[pl.ds(0, NZ - 1)]
     stats = remote(others, others, ss.at[0], sr.at[0], (x, wrap(z + 1, NZ), y, hd))
+    for copy in started:
+        copy.wait_send()
+    started.clear()
+    pl.semaphore_wait(ready.at[1], len(heads_here))
     stats.wait_recv()
     every = [lse[k] for k in range(NZ)]
     peak = functools.reduce(jnp.maximum, every)
@@ -306,6 +326,7 @@
             vmem((BLOCKS, 1, KEYS), f32),
             vmem((NH, NX, NY, 1, KEYS), f32),
             dma((6,)),
+            pltpu.SemaphoreType.REGULAR((2,)),
             dma((3 * BLOCKS - 1,)), dma((3, NX, NY)),
             dma((len(PLANE),)), dma((NX, NY)),
             dma((5 * NX,)), dma((NZ, NX)),

time: 43.3 us -> 41.3 us (0.954)
  Pallas kernels: 40.6 us -> 38.6 us
    pallas_call x1, Pallas kernels: 40.6 us -> 38.6 us  [body(): pl.pallas_call(kernel, out_shape=(jax.ShapeDtypeStruct((2, KVH // NH, KEY...]
where the time goes in v4:
time: 41.3 us; the launch traced here: 41.1 us
  Pallas kernels  38.6 us (93%)
  local copies, waits for them, and re-layouts  1.85 us (4%)
  between operations  0.65 us (2%)
    pallas_call x1, Pallas kernels, body(): pl.pallas_call(kernel, out_shape=(jax.ShapeDtypeStruct((2, KVH // NH, KEY...  38.6 us
    unnamed x4, local copies, waits for them, and re-layouts  1.85 us

profile of v4, /device:TPU:1, one launch (start us, length us, event | category | flops | bytes accessed | tf_op | source)
XLA Modules:
  0.0 41.1 jit_solution(3280921720390629220)
XLA Ops:
  0.6 38.6 %key_scores.1 = (f32[2,2,256]{2,1,0:T(2,128)}, f32[2,256]{1,0:T(2,128)}) custom-call(s32[2]{0:T(128)} %len_hbm.1, s32[2]{0:T(128)} %start_hbm.1, bf16[2,8,2048]{2,1,0:T(8,128)(2,1)} %q_hbm.1, bf16[2,256,256]{2,1,0:T(8,128)(2,1)} %k_hbm.1), custom_call_target="tpu_custom_call" | custom-call | tf_op jit(solution)/shard_map/key_scores/pallas_call | solution.py:306
  39.3 0.0 copy-start
  39.3 1.3 %copy.8 = f32[2,2,256]{2,1,0:T(2,128)} copy(f32[2,2,256]{2,1,0:T(2,128)} %get-tuple-element.4) | data formatting | bytes 8192
  40.6 0.0 copy-done
  40.6 0.6 %copy.9 = f32[2,256]{1,0:T(2,128)} copy(f32[2,256]{1,0:T(2,128)S(1)} %copy-done) | data formatting | bytes 4096
Async XLA Ops:
  39.3 1.3 %copy-start = (f32[2,256]{1,0:T(2,128)S(1)}, f32[2,256]{1,0:T(2,128)}, u32[]{:S(2)}) copy-start(f32[2,256]{1,0:T(2,128)} %get-tuple-element.5) | copy-start | bytes 6148

commit v5 on v4

--- a/solution.py
+++ b/solution.py
@@ -21,6 +21,8 @@
 HALF = H // KVH // NY
 ROWS = NX * NY * TOK * HALF
 BLOCKS = NX * NY
+TOKENS = BLOCKS * TOK
+SHARE = D // TOKENS
 FILL = -1e30
 SCALE2 = D**-0.5 * math.log2(math.e)
 MESH = pl.DeviceIdType.MESH
@@ -29,7 +31,8 @@
 ARRIVAL = {off: j for j, off in enumerate(OFFSETS)}
 STRIDES = (0, 1, 3, 2)
 NEAR = (0, 1, -1)
-FORWARD_AT = (2, 2, 2, 2)
+GROUPS = ((2,), (-2,), (3,), (-3,), (4,))
+FORWARD_AT = (4, 4, 4, 4)
 KEY_ORDER = ((0, 1), (3, 0), (1, 0), (3, 1), (1, 1), (2, 0), (2, 1))
 FIRST_KEYS = KEY_ORDER[:3]
 
@@ -40,7 +43,7 @@
 
 def kernel(
     len_hbm, start_hbm, q_hbm, k_hbm, key_out, tok_out,
-    len_ref, start_ref, qloc, kloc, qbuf, kbuf, sbuf, thr, msub, lsub, lse, part, got,
+    len_ref, start_ref, qloc, kloc, qbuf, kbuf, sbuf, barred, hot, msub, lsub, lse, part, got,
     loc_sem, ready, qs, qr, ks, kr, zs, zr, ss, sr, ps, pr,
 ):
     x, z, y, hd = (lax.axis_index(a) for a in AXES)
@@ -136,10 +139,24 @@
     b = x // 2
     start_pos = start_ref[b]
     first_pos = len_ref[b] - QLEN
-    for px in range(NX):
-        for py in range(NY):
-            pos = ((px * NZ + z) * NY + py) * KEYS + lax.broadcasted_iota(jnp.int32, (KEYS, D), 0)
-            thr[px * NY + py] = jnp.where(pos >= start_pos, pos, jnp.int32(2**30))
+    lane = lax.broadcasted_iota(jnp.int32, (1, D), 1)
+    token = lax.rem(lane, TOKENS)
+    inner = NY * TOK
+    lane_pos = first_pos + (token // inner) * (NZ * inner) + lax.rem(token, inner) + (lane // TOKENS) * inner
+
+    def mask(n, carry):
+        pos = (((n // NY) * NZ + z) * NY + lax.rem(n, NY)) * KEYS
+        pos = pos + lax.broadcasted_iota(jnp.int32, (KEYS, D), 0)
+        limit = jnp.where(pos >= start_pos, pos, jnp.int32(2**30))
+        for m in range(NZ // SHARE):
+            barred[m, n] = jnp.where(limit <= lane_pos + m * SHARE * inner, 0.0, FILL).astype(bf16)
+        return carry
+
+    lax.fori_loop(0, BLOCKS, mask, 0)
+    row = lax.rem(lax.broadcasted_iota(jnp.int32, (ROWS, D), 0), TOKENS)
+    for m in range(SHARE):
+        column = lax.broadcasted_iota(jnp.int32, (ROWS, D), 1) - m * TOKENS
+        hot[m] = jnp.where(row == column, 1.0, 0.0).astype(bf16)
 
     def z_copy(off, i, dz, n):
         slot, px = wrap(z + off, NZ), wrap(x + STRIDES[i], NX)
@@ -165,9 +182,11 @@
     def z_forward(i):
         for side in (1, -1):
             z_wait(side * 2, i)
-            if (i % 2 == 0) == (side == 1):
-                z_start(side * 2, i, -2 * side)
             z_start(side * 2, i, -side)
+        if i == NX - 1:
+            for k in range(NX):
+                side = 1 if k % 2 == 0 else -1
+                z_start(side * 2, k, -2 * side)
 
     for i, dx in enumerate(STRIDES):
         for side in (1, -1):
@@ -179,14 +198,11 @@
     def rows_of(c):
         wide = qbuf[c].astype(f32).reshape(BLOCKS * TOK, HALF * D)
         q = jnp.concatenate([wide[:, h * D:(h + 1) * D] for h in range(HALF)], axis=0).astype(bf16)
-        lane = lax.rem(lax.broadcasted_iota(jnp.int32, (1, ROWS), 1), BLOCKS * TOK)
-        inner = NY * TOK
-        return q, first_pos + (lane // inner) * (NZ * inner) + c * inner + lax.rem(lane, inner)
-
-    def score(c, q, query_pos, n):
-        s = lax.dot_general(kbuf[n], q, (((1,), (1,)), ((), ())), preferred_element_type=f32)
-        limit = thr[n]
-        s = jnp.where(jnp.concatenate([limit, limit], axis=1) <= query_pos, s, FILL)
+        return jnp.concatenate([q, hot[lax.rem(c, SHARE)]], axis=1)
+
+    def score(c, q, n):
+        k = jnp.concatenate([kbuf[n], barred[c // SHARE, n]], axis=1)
+        s = lax.dot_general(k, q, (((1,), (1,)), ((), ())), preferred_element_type=f32)
         top = jnp.max(s, axis=0, keepdims=True)
         e = jnp.exp2((s - top) * SCALE2)
         sbuf[c, n] = e
@@ -199,28 +215,28 @@
         total = jnp.sum(lsub[c] * jnp.exp2(tops - top), axis=0, keepdims=True)
         lse[z, pl.ds(c, 1), :] = top + jnp.log2(total)
 
-    near = [(wrap(z + off, NZ),) + rows_of(wrap(z + off, NZ)) for off in NEAR]
+    near = [(wrap(z + off, NZ), rows_of(wrap(z + off, NZ))) for off in NEAR]
     for n, (dx, dy) in enumerate(((0, 0),) + KEY_ORDER):
         px, py = wrap(x + dx, NX), wrap(y + dy, NY)
         if n > 0:
             remote(
                 keys_of(kloc, px), kbuf.at[px * NY + py], ks.at[0], kr.at[px, py], (px, z, py, hd)
             ).wait_recv()
-        for c, q, query_pos in near:
-            score(c, q, query_pos, px * NY + py)
+        for c, q in near:
+            score(c, q, px * NY + py)
         for i in range(NX):
             if n == FORWARD_AT[i]:
                 z_forward(i)
-    for offs in ((2, -2), (3, -3), (4,)):
+    for offs in GROUPS:
         for off in offs:
             if abs(off) > 2:
                 for i in range(NX):
                     z_wait(off, i)
-        far = [(wrap(z + off, NZ),) + rows_of(wrap(z + off, NZ)) for off in offs]
-        for c, q, query_pos in far:
+        far = [(wrap(z + off, NZ), rows_of(wrap(z + off, NZ))) for off in offs]
+        for c, q in far:
             for n in range(BLOCKS):
-                score(c, q, query_pos, n)
-        if offs == (2, -2):
+                score(c, q, n)
+        if 2 in offs:
             for off in NEAR:
                 merge(wrap(z + off, NZ))
         for off in offs:
@@ -319,7 +335,8 @@
             vmem((NZ, NX, NY, TOK, HALF * D), bf16),
             vmem((BLOCKS, KEYS, D), bf16),
             vmem((NZ, BLOCKS, KEYS, ROWS), f32),
-            vmem((BLOCKS, KEYS, D), jnp.int32),
+            vmem((NZ // SHARE, BLOCKS, KEYS, D), bf16),
+            vmem((SHARE, ROWS, D), bf16),
             vmem((NZ, BLOCKS, ROWS), f32),
             vmem((NZ, BLOCKS, ROWS), f32),
             vmem((NZ, NZ, ROWS), f32),

time: 41.3 us -> 40.3 us (0.976)
  Pallas kernels: 38.6 us -> 37.7 us
    pallas_call x1, Pallas kernels: 38.6 us -> 37.7 us  [body(): pl.pallas_call(kernel, out_shape=(jax.ShapeDtypeStruct((2, KVH // NH, KEY...]
where the time goes in v5:
time: 40.3 us; the launch traced here: 40.2 us
  Pallas kernels  37.7 us (94%)
  local copies, waits for them, and re-layouts  1.85 us (5%)
  between operations  0.65 us (2%)
    pallas_call x1, Pallas kernels, body(): pl.pallas_call(kernel, out_shape=(jax.ShapeDtypeStruct((2, KVH // NH, KEY...  37.7 us
    unnamed x4, local copies, waits for them, and re-layouts  1.85 us

profile of v5, /device:TPU:1, one launch (start us, length us, event | category | flops | bytes accessed | tf_op | source)
XLA Modules:
  0.0 40.2 jit_solution(10186261606397127801)
XLA Ops:
  0.6 37.7 %key_scores.1 = (f32[2,2,256]{2,1,0:T(2,128)}, f32[2,256]{1,0:T(2,128)}) custom-call(s32[2]{0:T(128)} %len_hbm.1, s32[2]{0:T(128)} %start_hbm.1, bf16[2,8,2048]{2,1,0:T(8,128)(2,1)} %q_hbm.1, bf16[2,256,256]{2,1,0:T(8,128)(2,1)} %k_hbm.1), custom_call_target="tpu_custom_call" | custom-call | tf_op jit(solution)/shard_map/key_scores/pallas_call | solution.py:322
  38.3 0.0 copy-start
  38.3 1.3 %copy.8 = f32[2,2,256]{2,1,0:T(2,128)} copy(f32[2,2,256]{2,1,0:T(2,128)} %get-tuple-element.4) | data formatting | bytes 8192
  39.6 0.0 copy-done
  39.6 0.6 %copy.9 = f32[2,256]{1,0:T(2,128)} copy(f32[2,256]{1,0:T(2,128)S(1)} %copy-done) | data formatting | bytes 4096
Async XLA Ops:
  38.3 1.3 %copy-start = (f32[2,256]{1,0:T(2,128)S(1)}, f32[2,256]{1,0:T(2,128)}, u32[]{:S(2)}) copy-start(f32[2,256]{1,0:T(2,128)} %get-tuple-element.5) | copy-start | bytes 6148

commit v6 on v5

--- a/solution.py
+++ b/solution.py
@@ -280,7 +280,7 @@
         if (dx, dy) == (0, 0):
             got[hd, x, y] = sums
         part[px * NY + py] = sums
-        for dh in (2, 3, 1, 0):
+        for dh in (3, 1, 2, 0):
             if (dx, dy, dh) != (0, 0, 0):
                 start(remote(
                     part.at[px * NY + py], got.at[hd, x, y], ps.at[0], pr.at[0],

time: 40.3 us -> 40.2 us (level)
  no operation moved by 1% of the time
where the time goes in v6:
time: 40.2 us; the launch traced here: 40.1 us
  Pallas kernels  37.6 us (94%)
  local copies, waits for them, and re-layouts  1.85 us (5%)
  between operations  0.65 us (2%)
    pallas_call x1, Pallas kernels, body(): pl.pallas_call(kernel, out_shape=(jax.ShapeDtypeStruct((2, KVH // NH, KEY...  37.6 us
    unnamed x4, local copies, waits for them, and re-layouts  1.85 us

profile of v6, /device:TPU:1, one launch (start us, length us, event | category | flops | bytes accessed | tf_op | source)
XLA Modules:
  0.0 40.1 jit_solution(10134934891740039569)
XLA Ops:
  0.6 37.6 %key_scores.1 = (f32[2,2,256]{2,1,0:T(2,128)}, f32[2,256]{1,0:T(2,128)}) custom-call(s32[2]{0:T(128)} %len_hbm.1, s32[2]{0:T(128)} %start_hbm.1, bf16[2,8,2048]{2,1,0:T(8,128)(2,1)} %q_hbm.1, bf16[2,256,256]{2,1,0:T(8,128)(2,1)} %k_hbm.1), custom_call_target="tpu_custom_call" | custom-call | tf_op jit(solution)/shard_map/key_scores/pallas_call | solution.py:322
  38.2 0.0 copy-start
  38.2 1.3 %copy.8 = f32[2,2,256]{2,1,0:T(2,128)} copy(f32[2,2,256]{2,1,0:T(2,128)} %get-tuple-element.4) | data formatting | bytes 8192
  39.5 0.0 copy-done
  39.5 0.6 %copy.9 = f32[2,256]{1,0:T(2,128)} copy(f32[2,256]{1,0:T(2,128)S(1)} %copy-done) | data formatting | bytes 4096
Async XLA Ops:
  38.2 1.3 %copy-start = (f32[2,256]{1,0:T(2,128)S(1)}, f32[2,256]{1,0:T(2,128)}, u32[]{:S(2)}) copy-start(f32[2,256]{1,0:T(2,128)} %get-tuple-element.5) | copy-start | bytes 6148

commit v7 on v5

--- a/solution.py
+++ b/solution.py
@@ -30,6 +30,7 @@
 OFFSETS = (0, 1, -1, 2, -2, 3, -3, 4)
 ARRIVAL = {off: j for j, off in enumerate(OFFSETS)}
 STRIDES = (0, 1, 3, 2)
+EARLY = 5
 NEAR = (0, 1, -1)
 GROUPS = ((2,), (-2,), (3,), (-3,), (4,))
 FORWARD_AT = (4, 4, 4, 4)
@@ -43,7 +44,7 @@
 
 def kernel(
     len_hbm, start_hbm, q_hbm, k_hbm, key_out, tok_out,
-    len_ref, start_ref, qloc, kloc, qbuf, kbuf, sbuf, barred, hot, msub, lsub, lse, part, got,
+    len_ref, start_ref, qloc, kloc, qbuf, kbuf, sbuf, barred, hot, msub, lsub, early, late, part, got,
     loc_sem, ready, qs, qr, ks, kr, zs, zr, ss, sr, ps, pr,
 ):
     x, z, y, hd = (lax.axis_index(a) for a in AXES)
@@ -209,11 +210,21 @@
         msub[c, pl.ds(n, 1), :] = top
         lsub[c, pl.ds(n, 1), :] = jnp.sum(e, axis=0, keepdims=True)
 
-    def merge(c):
+    def merge(off):
+        c, j = wrap(z + off, NZ), ARRIVAL[off]
         tops = msub[c] * SCALE2
         top = jnp.max(tops, axis=0, keepdims=True)
         total = jnp.sum(lsub[c] * jnp.exp2(tops - top), axis=0, keepdims=True)
-        lse[z, pl.ds(c, 1), :] = top + jnp.log2(total)
+        if j < EARLY:
+            early[z, j] = top + jnp.log2(total)
+        else:
+            late[z, j - EARLY] = top + jnp.log2(total)
+
+    def send_stats(rows, k):
+        for dz in (4, 3, -3, 2, -2, 1, -1):
+            start(remote(rows.at[z], rows.at[z], ss.at[k], sr.at[k], (x, wrap(z + dz, NZ), y, hd)), False)
+        others = rows.at[pl.ds(0, NZ - 1)]
+        return remote(others, others, ss.at[k], sr.at[k], (x, wrap(z + 1, NZ), y, hd))
 
     near = [(wrap(z + off, NZ), rows_of(wrap(z + off, NZ))) for off in NEAR]
     for n, (dx, dy) in enumerate(((0, 0),) + KEY_ORDER):
@@ -232,30 +243,35 @@
             if abs(off) > 2:
                 for i in range(NX):
                     z_wait(off, i)
+            if off == 3:
+                stats_early = send_stats(early, 0)
         far = [(wrap(z + off, NZ), rows_of(wrap(z + off, NZ))) for off in offs]
         for c, q in far:
             for n in range(BLOCKS):
                 score(c, q, n)
         if 2 in offs:
             for off in NEAR:
-                merge(wrap(z + off, NZ))
+                merge(off)
         for off in offs:
-            merge(wrap(z + off, NZ))
-
-    for dz in (4, 3, -3, 2, -2, 1, -1):
-        start(remote(lse.at[z], lse.at[z], ss.at[0], sr.at[0], (x, wrap(z + dz, NZ), y, hd)), False)
-    others = lse.at[pl.ds(0, NZ - 1)]
-    stats = remote(others, others, ss.at[0], sr.at[0], (x, wrap(z + 1, NZ), y, hd))
+            merge(off)
+
+    stats = send_stats(late, 1)
     for copy in started:
         copy.wait_send()
     started.clear()
     pl.semaphore_wait(ready.at[1], len(heads_here))
+    stats_early.wait_recv()
     stats.wait_recv()
-    every = [lse[k] for k in range(NZ)]
-    peak = functools.reduce(jnp.maximum, every)
-    whole = peak + jnp.log2(sum(jnp.exp2(v - peak) for v in every))
-    for c in range(NZ):
-        msub[c] = jnp.exp2(msub[c] * SCALE2 - whole[c:c + 1])
+    for off in OFFSETS:
+        every = []
+        for dz in OFFSETS:
+            j = ARRIVAL[(off - dz + NZ // 2 - 1) % NZ - NZ // 2 + 1]
+            source = wrap(z + dz, NZ)
+            every.append(early[source, j] if j < EARLY else late[source, j - EARLY])
+        peak = functools.reduce(jnp.maximum, every)
+        whole = peak + jnp.log2(sum(jnp.exp2(v - peak) for v in every))
+        c = wrap(z + off, NZ)
+        msub[c] = jnp.exp2(msub[c] * SCALE2 - whole)
 
     ones = jnp.ones((16, 2 * D), bf16)
 
@@ -311,7 +327,7 @@
             pair = request * heads + g
             key_out[request, g:g + 1] = got[hd, pair, 0] + got[hd, pair, 1]
 
-    for copy in started + [stats, returned]:
+    for copy in started + [stats_early, stats, returned]:
         copy.wait_send()
 
 
@@ -339,7 +355,8 @@
             vmem((SHARE, ROWS, D), bf16),
             vmem((NZ, BLOCKS, ROWS), f32),
             vmem((NZ, BLOCKS, ROWS), f32),
-            vmem((NZ, NZ, ROWS), f32),
+            vmem((NZ, EARLY, 1, ROWS), f32),
+            vmem((NZ, NZ - EARLY, 1, ROWS), f32),
             vmem((BLOCKS, 1, KEYS), f32),
             vmem((NH, NX, NY, 1, KEYS), f32),
             dma((6,)),
@@ -347,7 +364,7 @@
             dma((3 * BLOCKS - 1,)), dma((3, NX, NY)),
             dma((len(PLANE),)), dma((NX, NY)),
             dma((5 * NX,)), dma((NZ, NX)),
-            dma((1,)), dma((1,)),
+            dma((2,)), dma((2,)),
             dma((1,)), dma((1,)),
         ],
         compiler_params=pltpu.CompilerParams(

time: 40.3 us -> 40.4 us (level)
  no operation moved by 1% of the time
where the time goes in v7:
time: 40.4 us; the launch traced here: 40.3 us
  Pallas kernels  37.8 us (94%)
  local copies, waits for them, and re-layouts  1.85 us (5%)
  between operations  0.65 us (2%)
    pallas_call x1, Pallas kernels, body(): pl.pallas_call(kernel, out_shape=(jax.ShapeDtypeStruct((2, KVH // NH, KEY...  37.8 us
    unnamed x4, local copies, waits for them, and re-layouts  1.85 us

profile of v7, /device:TPU:1, one launch (start us, length us, event | category | flops | bytes accessed | tf_op | source)
XLA Modules:
  0.0 40.3 jit_solution(5880770091068067357)
XLA Ops:
  0.6 37.8 %key_scores.1 = (f32[2,2,256]{2,1,0:T(2,128)}, f32[2,256]{1,0:T(2,128)}) custom-call(s32[2]{0:T(128)} %len_hbm.1, s32[2]{0:T(128)} %start_hbm.1, bf16[2,8,2048]{2,1,0:T(8,128)(2,1)} %q_hbm.1, bf16[2,256,256]{2,1,0:T(8,128)(2,1)} %k_hbm.1), custom_call_target="tpu_custom_call" | custom-call | tf_op jit(solution)/shard_map/key_scores/pallas_call | solution.py:338
  38.5 0.0 copy-start
  38.5 1.3 %copy.8 = f32[2,2,256]{2,1,0:T(2,128)} copy(f32[2,2,256]{2,1,0:T(2,128)} %get-tuple-element.4) | data formatting | bytes 8192
  39.7 0.0 copy-done
  39.7 0.6 %copy.9 = f32[2,256]{1,0:T(2,128)} copy(f32[2,256]{1,0:T(2,128)S(1)} %copy-done) | data formatting | bytes 4096
Async XLA Ops:
  38.5 1.3 %copy-start = (f32[2,256]{1,0:T(2,128)S(1)}, f32[2,256]{1,0:T(2,128)}, u32[]{:S(2)}) copy-start(f32[2,256]{1,0:T(2,128)} %get-tuple-element.5) | copy-start | bytes 6148
